TPU v7x, 256 devices: a whole 4x4x8 slice. The times are simulated.
256 devices in a mesh: grid: 32 (over y, x, core), rows: 8 (over z).
Axes of the slice: x: 4, y: 4, z: 8, core: 2. Of those that a mesh axis runs over, the one named last changes fastest.
Arguments:
- density: bfloat16 [32, 128, 4096], P(None, 'rows', 'grid'), as said below
- basis_values: bfloat16 [64, 16, 128, 512], P('grid', None, 'rows'), may hold values from -0.59765625 to 0.59765625
- grid_points: float32 [64, 3, 512], P('grid'), may hold values from -4 to 4
- grid_weights: float32 [64, 512], P('grid'), may hold values from 0.05 to 1
- screened_blocks: int32 [64, 16], P('grid'), may hold values from 0 to 31, as said below
Outputs:
- exchange: float32 [32, 128, 4096], P(None, 'rows', 'grid')
Inputs may be any that keep to these rules, and one draw needn't show every extreme that they name: density is symmetric: density[a, i, b * 128 + j] equals density[b, j, a * 128 + i]. `screened_blocks`: each row holds 16 distinct block numbers.
All inputs are finite; a program needn't handle non-finite values.
Results may differ from a plain program's by a relative error of at most 0.00055.
The roundings to bfloat16 on the way count: a program that leaves them out, or rounds other values in their place, can miss the bound.
Values may be sent and summed in bfloat16 or wider, within the bound.
A program may use at most 64 MiB of HBM per device.

v0:
```python
import jax
import jax.numpy as jnp
from jax import lax
from jax.sharding import PartitionSpec as P


def copy_for_each(shard, axis):
    copies = jnp.broadcast_to(shard, (lax.axis_size(axis), *shard.shape))
    return lax.all_to_all(copies, axis, split_axis=0, concat_axis=0, tiled=True)


def joined_along(blocks, dim):
    shape = list(blocks.shape[1:])
    shape[dim] *= blocks.shape[0]
    return jnp.moveaxis(blocks, 0, dim).reshape(shape)


def gather_directly(shard, axis, dim):
    blocks = copy_for_each(shard, axis)
    return joined_along(blocks, dim)


def body(density, basis_values, grid_points, grid_weights, screened_blocks):
    nblocks = density.shape[0]
    rows_mine = density.shape[1]
    block_size = rows_mine * lax.axis_size("rows")
    nbasis = nblocks * block_size
    nsig = basis_values.shape[1]
    npoints = basis_values.shape[3]
    stripe = lax.all_gather(density, "grid", axis=2, tiled=True)
    totals = jnp.zeros((nblocks, rows_mine, nblocks, block_size), jnp.float32)
    for batch_index in range(basis_values.shape[0]):
        blocks = screened_blocks[batch_index]
        row_pick = jnp.take(stripe, blocks, axis=0).reshape(nsig * rows_mine, nblocks, block_size)
        chosen = jnp.take(row_pick, blocks, axis=1)
        local_values = basis_values[batch_index]
        x_mine = local_values.reshape(nsig * rows_mine, npoints)
        fsum = jnp.einsum(
            "mtk,tkp->mp",
            chosen,
            gather_directly(local_values, "rows", 1),
            preferred_element_type=jnp.float32,
        )
        fmat = fsum.astype(jnp.bfloat16)
        intersection_part = lax.dot_general(
            x_mine, fmat, (((0,), (0,)), ((), ())), preferred_element_type=jnp.float32
        )
        intersection = lax.psum(intersection_part, "rows")
        places = grid_points[batch_index]
        weights = grid_weights[batch_index]
        diffs = places[:, :, None] - places[:, None, :]
        kern = 1.0 / jnp.sqrt(jnp.sum(diffs * diffs, axis=0) + 0.5)
        mixed = (weights[:, None] * kern * intersection).astype(jnp.bfloat16)
        potential = (
            jnp.dot(x_mine, mixed, preferred_element_type=jnp.float32) * weights[None, :]
        ).astype(jnp.bfloat16)
        potential = potential.reshape(nsig, rows_mine, npoints)
        block_k = jnp.einsum(
            "mp,tkp->mtk",
            x_mine,
            lax.all_gather(potential, "rows", axis=1, tiled=True),
            preferred_element_type=jnp.float32,
        )
        block_k = block_k.reshape(nsig, rows_mine, nsig, block_size)
        totals = totals.at[blocks[:, None], :, blocks[None, :], :].add(
            block_k.transpose(0, 2, 1, 3)
        )
    return lax.psum_scatter(
        totals.reshape(nblocks, rows_mine, nbasis), "grid", scatter_dimension=2, tiled=True
    )


def solution(mesh):
    placed = (
        P(None, "rows", "grid"),
        P("grid", None, "rows", None),
        P("grid", None, None),
        P("grid", None),
        P("grid", None),
    )
    return jax.shard_map(
        body, mesh=mesh, in_specs=placed, out_specs=P(None, "rows", "grid"), check_vma=False
    )
```

profile of v0, /device:TPU:2, one launch (start us, length us, event | category | flops | bytes accessed | tf_op | source)
XLA Modules:
  0.0 494.6 jit_solution(1196830963108560420)
XLA Ops:
  6.5 0.7 all-gather.4.cloned.1.call-update
  7.3 1.1 slice_bitcast_fusion
  8.6 59.6 %all_to_all.10 = bf16[8,16,16,512]{3,2,1,0:T(8,128)(2,1)} all-to-all(bf16[8,16,16,512]{3,2,1,0:T(8,128)(2,1)S(1)} %broadcast_in_dim.59), channel_id=1, replica_groups=mesh['grid'=32,'rows'=8] {'rows'}, dimensions={0} | all-to-all | bytes 4194304 | tf_op jit(solution)/shard_map/all_to_all | solution.py:9
  68.2 1.6 broadcast_in_dim.55
  69.8 3.7 all-to-all-start
  73.7 3.2 copy.34
  76.8 46.5 %all-to-all-done = bf16[8,16,16,512]{3,2,1,0:T(8,128)(2,1)S(1)} async-done(((bf16[8,16,16,512]{3,2,1,0:T(8,128)(2,1)}), bf16[8,16,16,512]{3,2,1,0:T(8,128)(2,1)S(1)}, u32[]{:S(2)}, u32[]{:S(2)}) %all-to-all-start) | async-done | bytes 2097184 | tf_op jit(solution)/shard_map/all_to_all | solution.py:9
  123.3 1.6 copy.29
  124.9 2.9 gather_fusion.2
  128.5 0.8 copy.33
  129.3 1.7 gather_fusion.3
  131.1 2.9 gather_fusion
  134.7 0.8 copy.28
  135.5 1.7 gather_fusion.1
  137.2 4.1 convolution_bitcast_fusion.2
  141.3 3.3 convolution_bitcast_fusion.3
  146.0 77.3 %all-reduce.3.cloned.1.call-done = (f32[512,512]{0,1:T(8,128)}, f32[512,512]{0,1:T(8,128)}) async-done(((f32[512,512]{0,1:T(8,128)}, f32[512,512]{0,1:T(8,128)}), (f32[512,512]{0,1:T(8,128)}, f32[512,512]{0,1:T(8,128)})) %all-reduce.3.cloned.1.call-update) | async-done | bytes 2097168 | tf_op jit(solution)/shard_map/psum | solution.py:48
  223.3 2.3 fusion
  226.4 2.3 fusion.1
  229.3 36.4 %all-gather.6.cloned.1.call-done = bf16[16,128,512]{2,1,0:T(8,128)(2,1)} async-done(((bf16[16,16,512]{2,1,0:T(8,128)(2,1)}), bf16[16,128,512]{2,1,0:T(8,128)(2,1)}) %all-gather.6.cloned.1.call-update) | async-done | bytes 2097168 | tf_op jit(solution)/shard_map/all_gather | solution.py:61
  265.7 2.3 convolution_bitcast_fusion.1
  268.0 2.0 copy.30
  270.0 2.3 copy.31
  272.2 34.5 %all-gather.8.cloned.1.call-done = bf16[16,128,512]{2,1,0:T(8,128)(2,1)} async-done(((bf16[16,16,512]{2,1,0:T(8,128)(2,1)}), bf16[16,128,512]{2,1,0:T(8,128)(2,1)}) %all-gather.8.cloned.1.call-update) | async-done | bytes 2097168 | tf_op jit(solution)/shard_map/all_gather | solution.py:61
  306.8 3.6 convolution_bitcast_fusion
  310.4 3.1 copy.35
  313.5 3.6 copy.36
  317.1 4.2 broadcast_in_dim.51
  321.3 28.4 %scatter_fusion = f32[32,16,32,128]{3,1,2,0:T(8,128)} fusion(f32[32,16,32,128]{3,1,2,0:T(8,128)} %broadcast_in_dim.51, s32[256]{0:T(256)S(1)} %reshape.140, f32[256,16,128]{2,1,0:T(8,128)S(1)} %bitcast.107), kind=kCustom, calls=%fused_computation.4 | custom fusion | flops 524288 | bytes 6293504 | tf_op jit(solution)/shard_map/scatter-add | solution.py:65
  349.7 31.8 %scatter_fusion.1 = f32[32,16,32,128]{3,1,2,0:T(8,128)} fusion(f32[32,16,32,128]{3,1,2,0:T(8,128)} %scatter_fusion, s32[256]{0:T(256)S(1)} %reshape.146, f32[256,16,128]{2,1,0:T(8,128)} %bitcast.108), kind=kCustom, calls=%fused_computation.5 | custom fusion | flops 524288 | bytes 6293504 | tf_op jit(solution)/shard_map/scatter-add | solution.py:65
  381.5 7.8 %copy_bitcast_fusion = f32[32,16,4096]{2,1,0:T(8,128)} fusion(f32[32,16,32,128]{3,1,2,0:T(8,128)} %scatter_fusion.1), kind=kLoop, calls=%fused_computation.6 | loop fusion | bytes 16777216 | tf_op jit(solution)/shard_map/reshape | solution.py:69
  389.3 98.8 %reduce-scatter.2.cloned.1.call-done = f32[32,16,128]{2,1,0:T(8,128)} async-done(((f32[32,16,4096]{2,1,0:T(8,128)}), f32[32,16,128]{2,1,0:T(8,128)}) %reduce-scatter.2.cloned.1.call-update) | async-done | bytes 262160 | tf_op jit(solution)/shard_map/reduce_scatter | solution.py:68
  (41 shorter events, 4.5 us)
Async XLA Ops:
  6.5 118.4 %all-gather.4.cloned.1.call-start = ((), (), s32[]{:S(2)}) async-start(), calls=%async_computation.3 | async-start | bytes 4325376 | tf_op jit(solution)/shard_map/all_gather | solution.py:30
  69.8 3.8 copy-start.3
  69.8 53.5 %all-to-all-start = ((bf16[8,16,16,512]{3,2,1,0:T(8,128)(2,1)}), bf16[8,16,16,512]{3,2,1,0:T(8,128)(2,1)S(1)}, u32[]{:S(2)}, u32[]{:S(2)}) async-start(bf16[8,16,16,512]{3,2,1,0:T(8,128)(2,1)} %broadcast_in_dim.55), calls=%async_computation | async-start | bytes 4194304 | tf_op jit(solution)/shard_map/all_to_all | solution.py:9
  73.5 149.8 %all-reduce.3.cloned.1.call-start = ((), (), s32[]{:S(2)}) async-start(), calls=%async_computation.7 | async-start | bytes 4194304 | tf_op jit(solution)/shard_map/psum | solution.py:48
  137.2 4.1 copy-start
  144.6 0.7 copy-start.1
  144.6 1.4 copy-start.2
  144.6 121.1 %all-gather.6.cloned.1.call-start = ((), (), s32[]{:S(2)}) async-start(), calls=%async_computation.4 | async-start | bytes 2359296 | tf_op jit(solution)/shard_map/all_gather | solution.py:61
  225.7 81.1 %all-gather.8.cloned.1.call-start = ((), (), s32[]{:S(2)}) async-start(), calls=%async_computation.5 | async-start | bytes 2359296 | tf_op jit(solution)/shard_map/all_gather | solution.py:61
  228.7 259.3 %reduce-scatter.2.cloned.1.call-start = ((), (), s32[]{:S(2)}) async-start(), calls=%async_computation.6 | async-start | bytes 8650752 | tf_op jit(solution)/shard_map/reduce_scatter | solution.py:68
Sparse Core Ops, SparseCore 0:
  9.8 56.2 all-gather.3
  144.7 78.5 all-reduce.2
  225.8 39.8 all-gather.5
  267.3 39.4 all-gather.7
  389.4 98.5 reduce-scatter.1
where the time goes:
time: 496 us; the launch traced here: 495 us
  waiting for transfers between devices  294 us (59%)
  other arithmetic  61.6 us (12%)
  blocking collectives  59.6 us (12%)
  local copies, waits for them, and re-layouts  43.8 us (9%)
  matrix products  17.9 us (4%)
  between operations  13.4 us (3%)
    reduce_scatter x1, waiting for transfers between devices, body(): lax.psum_scatter(totals.reshape(nblocks, rows_mine, nbasis), 'grid', scat...  98.8 us
    psum x1, waiting for transfers between devices, body(): intersection = lax.psum(intersection_part, 'rows')  77.3 us
    all_gather x2, waiting for transfers between devices, body(): lax.all_gather(potential, 'rows', axis=1, tiled=True)  70.9 us
    scatter-add x2, other arithmetic, body(): totals.at[blocks[:, None], :, blocks[None, :], :]  60.2 us
    all_to_all x1, blocking collectives, copy_for_each(): return lax.all_to_all(copies, axis, split_axis=0, concat_axis=0, tiled=True)  59.6 us
    all_to_all x1, waiting for transfers between devices, copy_for_each(): return lax.all_to_all(copies, axis, split_axis=0, concat_axis=0, tiled=True)  46.5 us
  transfers between devices with their start and end apart: 6, of which 5 were waited for; matrix products, arithmetic and copies ran while one was open for 4% of the time, Pallas kernels for 0%

commit v1 on v0

--- a/solution.py
+++ b/solution.py
@@ -2,6 +2,17 @@
 import jax.numpy as jnp
 from jax import lax
 from jax.sharding import PartitionSpec as P
+from jax.lax import axis_size, ppermute
+
+
+def render_points(piece_in):
+    chip_axis = "rows"
+    n_shards = axis_size(chip_axis)
+    e_next = lambda q_next: [(h, h ^ q_next) for h in range(n_shards)]
+    z = piece_in
+    for j in range(n_shards.bit_length() - 1):
+        z = z + ppermute(z, chip_axis, e_next(1 << j))
+    return z
 
 
 def copy_for_each(shard, axis):
@@ -45,7 +56,7 @@
         intersection_part = lax.dot_general(
             x_mine, fmat, (((0,), (0,)), ((), ())), preferred_element_type=jnp.float32
         )
-        intersection = lax.psum(intersection_part, "rows")
+        intersection = render_points(intersection_part)
         places = grid_points[batch_index]
         weights = grid_weights[batch_index]
         diffs = places[:, :, None] - places[:, None, :]

time: 496 us -> 618 us (1.25)
  waiting for transfers between devices: 294 us -> 385 us
  starting transfers between devices: 4.08 us -> 24.6 us
    ppermute x0 -> x6, waiting for transfers between devices: none -> 253 us  [render_points(): z = z + ppermute(z, chip_axis, e_next(1 << j))]
    psum x1 -> x0, waiting for transfers between devices: 77.3 us -> none  [body(): intersection = lax.psum(intersection_part, 'rows')]
    all_to_all x1, waiting for transfers between devices: 46.5 us -> 0.01 us  [copy_for_each(): return lax.all_to_all(copies, axis, split_axis=0, concat_axis=0, tiled=True)]
    all_gather x2, waiting for transfers between devices: 70.9 us -> 32.4 us  [body(): lax.all_gather(potential, 'rows', axis=1, tiled=True)]
    ppermute x0 -> x6, starting transfers between devices: none -> 20.7 us  [render_points(): z = z + ppermute(z, chip_axis, e_next(1 << j))]
  transfers between devices with their start and end apart: 6 -> 11, of which waited for: 5 -> 8; matrix products, arithmetic and copies ran while one was open for 4% -> 8% of each run, Pallas kernels for 0% -> 0%
where the time goes in v1:
time: 618 us; the launch traced here: 616 us
  waiting for transfers between devices  385 us (62%)
  other arithmetic  66.4 us (11%)
  blocking collectives  59.6 us (10%)
  local copies, waits for them, and re-layouts  49.9 us (8%)
  starting transfers between devices  24.6 us (4%)
  matrix products  17.4 us (3%)
  between operations  13.4 us (2%)
    ppermute x6, waiting for transfers between devices, render_points(): z = z + ppermute(z, chip_axis, e_next(1 << j))  253 us
    reduce_scatter x1, waiting for transfers between devices, body(): lax.psum_scatter(totals.reshape(nblocks, rows_mine, nbasis), 'grid', scat...  98.7 us
    scatter-add x2, other arithmetic, body(): totals.at[blocks[:, None], :, blocks[None, :], :]  60.2 us
    all_to_all x1, blocking collectives, copy_for_each(): return lax.all_to_all(copies, axis, split_axis=0, concat_axis=0, tiled=True)  59.6 us
    all_gather x2, waiting for transfers between devices, body(): lax.all_gather(potential, 'rows', axis=1, tiled=True)  32.4 us
    ppermute x6, starting transfers between devices, render_points(): z = z + ppermute(z, chip_axis, e_next(1 << j))  20.7 us
  transfers between devices with their start and end apart: 11, of which 8 were waited for; matrix products, arithmetic and copies ran while one was open for 8% of the time, Pallas kernels for 0%

profile of v1, /device:TPU:2, one launch (start us, length us, event | category | flops | bytes accessed | tf_op | source)
XLA Modules:
  0.0 616.1 jit_solution(948850153555150799)
XLA Ops:
  8.7 59.6 %all_to_all.10 = bf16[8,16,16,512]{3,2,1,0:T(8,128)(2,1)} all-to-all(bf16[8,16,16,512]{3,2,1,0:T(8,128)(2,1)S(1)} %broadcast_in_dim.59), channel_id=1, replica_groups=mesh['grid'=32,'rows'=8] {'rows'}, dimensions={0} | all-to-all | bytes 4194304 | tf_op jit(solution)/shard_map/all_to_all | solution.py:20
  69.9 3.7 all-to-all-start
  73.7 3.2 copy.34
  76.9 4.3 gather_fusion.2
  85.7 3.2 gather_fusion.3
  89.0 4.0 convolution_bitcast_fusion.2
  94.9 47.0 %collective-permute-done.3 = f32[512,512]{0,1:T(8,128)S(1)} collective-permute-done((f32[512,512]{0,1:T(8,128)}, f32[512,512]{0,1:T(8,128)S(1)}, u32[]{:S(2)}, u32[]{:S(2)}) %collective-permute-start.3) | collective-permute-done | bytes 1048608 | tf_op jit(solution)/shard_map/ppermute | solution.py:14
  143.3 2.5 collective-permute-start.4
  147.3 41.9 %collective-permute-done.4 = f32[512,512]{0,1:T(8,128)S(1)} collective-permute-done((f32[512,512]{0,1:T(8,128)S(1)}, f32[512,512]{0,1:T(8,128)S(1)}, u32[]{:S(2)}, u32[]{:S(2)}) %collective-permute-start.4) | collective-permute-done | bytes 1048608 | tf_op jit(solution)/shard_map/ppermute | solution.py:14
  189.4 6.3 %collective-permute-start.5 = (f32[512,512]{0,1:T(8,128)S(1)}, f32[512,512]{0,1:T(8,128)}, u32[]{:S(2)}, u32[]{:S(2)}) collective-permute-start(f32[512,512]{0,1:T(8,128)S(1)} %add.68), channel_id=1, source_target_pairs={{0,4},{1,5},{2,6},{3,7},{4,0},{5,1},{6,2},{7,3},{8,12},{9,13},{10,... | collective-permute-start | bytes 3145736 | tf_op jit(solution)/shard_map/ppermute | solution.py:14
  195.8 2.6 copy.32
  200.0 2.9 gather_fusion
  206.1 34.3 %collective-permute-done.5 = f32[512,512]{0,1:T(8,128)} collective-permute-done((f32[512,512]{0,1:T(8,128)S(1)}, f32[512,512]{0,1:T(8,128)}, u32[]{:S(2)}, u32[]{:S(2)}) %collective-permute-start.5) | collective-permute-done | bytes 1048608 | tf_op jit(solution)/shard_map/ppermute | solution.py:14
  240.4 2.7 fusion.1
  243.2 2.3 convolution_bitcast_fusion.3
  245.6 37.7 %collective-permute-done = f32[512,512]{0,1:T(8,128)S(1)} collective-permute-done((f32[512,512]{0,1:T(8,128)S(1)}, f32[512,512]{0,1:T(8,128)S(1)}, u32[]{:S(2)}, u32[]{:S(2)}) %collective-permute-start) | collective-permute-done | bytes 1048608 | tf_op jit(solution)/shard_map/ppermute | solution.py:14
  283.5 6.1 collective-permute-start.1
  289.6 46.1 %collective-permute-done.1 = f32[512,512]{0,1:T(8,128)S(1)} collective-permute-done((f32[512,512]{0,1:T(8,128)S(1)}, f32[512,512]{0,1:T(8,128)S(1)}, u32[]{:S(2)}, u32[]{:S(2)}) %collective-permute-start.1) | collective-permute-done | bytes 1048608 | tf_op jit(solution)/shard_map/ppermute | solution.py:14
  335.9 3.9 collective-permute-start.2
  340.5 46.0 %collective-permute-done.2 = f32[512,512]{0,1:T(8,128)} collective-permute-done((f32[512,512]{0,1:T(8,128)S(1)}, f32[512,512]{0,1:T(8,128)}, u32[]{:S(2)}, u32[]{:S(2)}) %collective-permute-start.2) | collective-permute-done | bytes 1048608 | tf_op jit(solution)/shard_map/ppermute | solution.py:14
  386.5 2.4 fusion
  389.3 2.3 convolution_bitcast_fusion
  393.6 2.3 copy.36
  395.9 32.4 %all-gather.6.cloned.1.call-done = bf16[16,128,512]{2,1,0:T(8,128)(2,1)} async-done(((bf16[16,16,512]{2,1,0:T(8,128)(2,1)}), bf16[16,128,512]{2,1,0:T(8,128)(2,1)}) %all-gather.6.cloned.1.call-update) | async-done | bytes 2097168 | tf_op jit(solution)/shard_map/all_gather | solution.py:72
  428.3 3.7 convolution_bitcast_fusion.1
  431.9 3.1 copy.30
  435.0 3.6 copy.31
  438.6 4.2 broadcast_in_dim.51
  442.8 31.8 %scatter_fusion = f32[32,16,32,128]{3,1,2,0:T(8,128)} fusion(f32[32,16,32,128]{3,1,2,0:T(8,128)} %broadcast_in_dim.51, s32[256]{0:T(256)S(1)} %reshape.140, f32[256,16,128]{2,1,0:T(8,128)} %bitcast.108), kind=kCustom, calls=%fused_computation.4 | custom fusion | flops 524288 | bytes 6293504 | tf_op jit(solution)/shard_map/scatter-add | solution.py:76
  474.7 28.4 %scatter_fusion.1 = f32[32,16,32,128]{3,1,2,0:T(8,128)} fusion(f32[32,16,32,128]{3,1,2,0:T(8,128)} %scatter_fusion, s32[256]{0:T(256)S(1)} %reshape.146, f32[256,16,128]{2,1,0:T(8,128)S(1)} %bitcast.107), kind=kCustom, calls=%fused_computation.5 | custom fusion | flops 524288 | bytes 6293504 | tf_op jit(solution)/shard_map/scatter-add | solution.py:76
  503.1 7.8 %copy_bitcast_fusion = f32[32,16,4096]{2,1,0:T(8,128)} fusion(f32[32,16,32,128]{3,1,2,0:T(8,128)} %scatter_fusion.1), kind=kLoop, calls=%fused_computation.6 | loop fusion | bytes 16777216 | tf_op jit(solution)/shard_map/reshape | solution.py:80
  510.9 98.7 %reduce-scatter.2.cloned.1.call-done = f32[32,16,128]{2,1,0:T(8,128)} async-done(((f32[32,16,4096]{2,1,0:T(8,128)}), f32[32,16,128]{2,1,0:T(8,128)}) %reduce-scatter.2.cloned.1.call-update) | async-done | bytes 262160 | tf_op jit(solution)/shard_map/reduce_scatter | solution.py:79
  (57 shorter events, 21.8 us)
Async XLA Ops:
  6.5 70.4 %all-gather.4.cloned.1.call-start = ((), (), s32[]{:S(2)}) async-start(), calls=%async_computation.3 | async-start | bytes 4325376 | tf_op jit(solution)/shard_map/all_gather | solution.py:41
  8.4 80.5 %copy-start = (bf16[1,16,16,512]{3,2,1,0:T(8,128)(2,1)}, bf16[1,16,16,512]{3,2,1,0:T(8,128)(2,1)S(1)}, u32[]{:S(2)}) copy-start(bf16[1,16,16,512]{3,2,1,0:T(8,128)(2,1)S(1)} %get-tuple-element.13) | copy-start | bytes 786436
  69.9 3.8 copy-start.5
  69.9 128.5 %all-to-all-start = ((bf16[8,16,16,512]{3,2,1,0:T(8,128)(2,1)}), bf16[8,16,16,512]{3,2,1,0:T(8,128)(2,1)S(1)}, u32[]{:S(2)}, u32[]{:S(2)}) async-start(bf16[8,16,16,512]{3,2,1,0:T(8,128)(2,1)} %broadcast_in_dim.55), calls=%async_computation | async-start | bytes 4194304 | tf_op jit(solution)/shard_map/all_to_all | solution.py:20
  73.6 315.7 %all-gather.8.cloned.1.call-start = ((), (), s32[]{:S(2)}) async-start(), calls=%async_computation.5 | async-start | bytes 2359296 | tf_op jit(solution)/shard_map/all_gather | solution.py:72
  93.0 52.8 %copy-start.3 = (f32[2,3,512]{2,0,1:T(2,128)S(1)}, f32[2,3,512]{2,0,1:T(2,128)}, u32[]{:S(2)}) copy-start(f32[2,3,512]{2,0,1:T(2,128)} %param.11) | copy-start | bytes 36868
  93.0 54.3 %copy-start.4 = (f32[2,512]{1,0:T(2,128)S(1)}, f32[2,512]{1,0:T(2,128)}, u32[]{:S(2)}) copy-start(f32[2,512]{1,0:T(2,128)} %param.12) | copy-start | bytes 12292
  93.0 48.9 %collective-permute-start.3 = (f32[512,512]{0,1:T(8,128)}, f32[512,512]{0,1:T(8,128)S(1)}, u32[]{:S(2)}, u32[]{:S(2)}) collective-permute-start(f32[512,512]{0,1:T(8,128)} %convolution_bitcast_fusion.2), channel_id=1, source_target_pairs={{0,1},{1,0},{2,3},{3,2},{4,5},{5,4},{6,7},{7,6},{8,9},{9,8},{10,11... | collective-permute-start | bytes 3145736 | tf_op jit(solution)/shard_map/ppermute | solution.py:14
  143.3 45.9 %collective-permute-start.4 = (f32[512,512]{0,1:T(8,128)S(1)}, f32[512,512]{0,1:T(8,128)S(1)}, u32[]{:S(2)}, u32[]{:S(2)}) collective-permute-start(f32[512,512]{0,1:T(8,128)S(1)} %add.67), channel_id=1, source_target_pairs={{0,2},{1,3},{2,0},{3,1},{4,6},{5,7},{6,4},{7,5},{8,10},{9,11},{10,... | collective-permute-start | bytes 3145736 | tf_op jit(solution)/shard_map/ppermute | solution.py:14
  189.4 50.9 %collective-permute-start.5 = (f32[512,512]{0,1:T(8,128)S(1)}, f32[512,512]{0,1:T(8,128)}, u32[]{:S(2)}, u32[]{:S(2)}) collective-permute-start(f32[512,512]{0,1:T(8,128)S(1)} %add.68), channel_id=1, source_target_pairs={{0,4},{1,5},{2,6},{3,7},{4,0},{5,1},{6,2},{7,3},{8,12},{9,13},{10,... | collective-permute-start | bytes 3145736 | tf_op jit(solution)/shard_map/ppermute | solution.py:14
  206.1 37.1 %copy-start.2 = (bf16[8,16,16,512]{3,2,0,1:T(8,128)(2,1)S(1)}, bf16[8,16,16,512]{3,2,0,1:T(8,128)(2,1)}, u32[]{:S(2)}) copy-start(bf16[8,16,16,512]{3,2,0,1:T(8,128)(2,1)} %copy.29) | copy-start | bytes 6291460
  243.1 185.1 %all-gather.6.cloned.1.call-start = ((), (), s32[]{:S(2)}) async-start(), calls=%async_computation.4 | async-start | bytes 2359296 | tf_op jit(solution)/shard_map/all_gather | solution.py:72
  245.5 37.8 %collective-permute-start = (f32[512,512]{0,1:T(8,128)S(1)}, f32[512,512]{0,1:T(8,128)S(1)}, u32[]{:S(2)}, u32[]{:S(2)}) collective-permute-start(f32[512,512]{0,1:T(8,128)S(1)} %convolution_bitcast_fusion.3), channel_id=1, source_target_pairs={{0,1},{1,0},{2,3},{3,2},{4,5},{5,4},{6,7},{7,6},{8,9},{9,8},{10,11... | collective-permute-start | bytes 3145736 | tf_op jit(solution)/shard_map/ppermute | solution.py:14
  283.5 52.2 %collective-permute-start.1 = (f32[512,512]{0,1:T(8,128)S(1)}, f32[512,512]{0,1:T(8,128)S(1)}, u32[]{:S(2)}, u32[]{:S(2)}) collective-permute-start(f32[512,512]{0,1:T(8,128)S(1)} %add.61), channel_id=1, source_target_pairs={{0,2},{1,3},{2,0},{3,1},{4,6},{5,7},{6,4},{7,5},{8,10},{9,11},{10,... | collective-permute-start | bytes 3145736 | tf_op jit(solution)/shard_map/ppermute | solution.py:14
  335.9 50.6 %collective-permute-start.2 = (f32[512,512]{0,1:T(8,128)S(1)}, f32[512,512]{0,1:T(8,128)}, u32[]{:S(2)}, u32[]{:S(2)}) collective-permute-start(f32[512,512]{0,1:T(8,128)S(1)} %add.62), channel_id=1, source_target_pairs={{0,4},{1,5},{2,6},{3,7},{4,0},{5,1},{6,2},{7,3},{8,12},{9,13},{10,... | collective-permute-start | bytes 3145736 | tf_op jit(solution)/shard_map/ppermute | solution.py:14
  340.5 48.8 %copy-start.1 = (bf16[1,16,16,512]{3,2,1,0:T(8,128)(2,1)S(1)}, bf16[1,16,16,512]{3,2,1,0:T(8,128)(2,1)}, u32[]{:S(2)}) copy-start(bf16[1,16,16,512]{3,2,1,0:T(8,128)(2,1)} %copy-done) | copy-start | bytes 786436
  388.9 220.6 %reduce-scatter.2.cloned.1.call-start = ((), (), s32[]{:S(2)}) async-start(), calls=%async_computation.6 | async-start | bytes 8650752 | tf_op jit(solution)/shard_map/reduce_scatter | solution.py:79
Sparse Core Ops, SparseCore 0:
  9.8 56.2 all-gather.3
  243.2 50.5 all-gather.7
  389.0 39.1 all-gather.5
  511.0 98.5 reduce-scatter.1
